TPU v7x, 32 devices: a whole 2x2x4 slice. The times are simulated.
32 devices in a mesh: gx: 4 (over y, core), gy: 8 (over z, x).
Axes of the slice: x: 2, y: 2, z: 4, core: 2. Of those that a mesh axis runs over, the one named last changes fastest.
Arguments:
- old_master: float32 [32, 128, 1536], P('gx', 'gy'), may hold values from -3 to 3
- old_first: float32 [32, 128, 1536], P('gx', 'gy'), may hold values from -3 to 3
- old_second: float32 [32, 128, 1536], P('gx', 'gy'), may hold values from 0.01 to 1
- new_grad: bfloat16 [32, 128, 1536], P(('gx', 'gy')), may hold values from -3072 to 3072
- counts: int32 [32, 32], P(None, ('gx', 'gy')), may hold values from 1 to 72, as said below
- old_owner: int32 [32], replicated, may hold values from 0 to 31, each once
- new_owner: int32 [32], replicated, may hold values from 0 to 31, each once
Outputs:
- new_master: float32 [32, 128, 1536], P(('gx', 'gy'))
- new_first: float32 [32, 128, 1536], P(('gx', 'gy'))
- new_second: float32 [32, 128, 1536], P(('gx', 'gy'))
Inputs may be any that keep to these rules, and one draw needn't show every extreme that they name: `old_owner`: every number of 0 to 31 appears once. `new_owner`: every number of 0 to 31 appears once. `counts`: every device routed at least one token to every expert.
All inputs are finite; a program needn't handle non-finite values.
Results may differ from a plain program's by a relative error of at most 0.0003.
Values sent between devices are 32-bit elements; how exact they have to be, the bound alone decides.
A program may use at most 64 MiB of HBM per device.

v0:
```python
import functools

import jax
import jax.numpy as jnp
from jax import lax
from jax.experimental import pallas as pl
from jax.experimental.pallas import tpu as pltpu
from jax.sharding import PartitionSpec as P

first_correction = 1.0 - 0.9**10
second_correction = 1.0 - 0.999**10
MESH = pl.DeviceIdType.MESH
LANES = 128
VMEM_GRANT = 10 << 20
SUBLANES = 8


def adam_step(master, first, second, grad, slot_count):
    scaled = grad.astype(jnp.float32) / slot_count
    new_first = 0.9 * first + 0.1 * scaled
    new_second = 0.999 * second + 0.001 * scaled * scaled
    step_dir = new_first / first_correction / (jnp.sqrt(new_second / second_correction) + 1e-08)
    new_master = master - 0.01 * (step_dir + 0.1 * master)
    return (new_master, new_first, new_second)


def reorder(block, groups_x, groups_y):
    total_rows = block.shape[1]
    piece = total_rows // (groups_x * groups_y)
    shaped = block.reshape(1, groups_x, groups_y, piece, block.shape[2])
    return shaped.transpose(0, 2, 1, 3, 4).reshape(1, total_rows, block.shape[2])


def plain_body(old_master, old_first, old_second, new_grad, counts, old_owner, new_owner):
    experts = old_owner.shape[0]
    groups_x = lax.axis_size("gx")
    groups_y = lax.axis_size("gy")
    my_slot = lax.axis_index("gx") * groups_y + lax.axis_index("gy")
    slots = jnp.arange(experts, dtype=jnp.int32)
    onehot = new_owner[:, None] == slots[None, :]
    source = jnp.sum(jnp.where(onehot, old_owner[:, None], 0), axis=0)
    local_counts = counts[:, 0].astype(jnp.float32)
    by_rows = tuple(
        lax.all_to_all(state, "gx", split_axis=1, concat_axis=0, tiled=True)
        for state in (old_master, old_first, old_second)
    )
    permuted = tuple((jnp.take(state, source, axis=0) for state in by_rows))
    landed = lax.all_to_all(permuted, ("gx", "gy"), split_axis=0, concat_axis=1, tiled=True)
    arrived = tuple((reorder(state, groups_x, groups_y) for state in landed))
    totals = lax.psum(local_counts, ("gx", "gy"))
    slot_count = jnp.sum(jnp.where(new_owner == my_slot, totals, jnp.float32(0.0)))
    return adam_step(arrived[0], arrived[1], arrived[2], new_grad, slot_count)


def rehome_kernel(dims, old_owner_hbm, new_owner_hbm, owner_row_hbm, count_row, old_m, old_f, old_s, *rest):
    groups_x, groups_y, experts, held, rows, tiles, span, pieces = dims
    chunks = len(pieces)
    outs, count_out = rest[:3], rest[3]
    by_rows = rest[4 : 4 + chunks]
    staged = rest[4 + chunks : 4 + 2 * chunks]
    ready = rest[4 + 2 * chunks : 4 + 3 * chunks]
    (
        source, old_owner, new_owner, owner_row, all_counts, small_sem, local_sem, self_sem,
        send1, recv1, send2, recv2, send_c, recv_c, row_in,
    ) = rest[4 + 3 * chunks :]
    olds = (old_m, old_f, old_s)
    devices = groups_x * groups_y
    splits = groups_x // tiles
    gx = lax.axis_index("gx")
    gy = lax.axis_index("gy")
    me = gx * groups_y + gy

    peers_x = [(gx + off) % groups_x for off in range(groups_x)]
    offsets = sorted(range(groups_y), key=lambda off: (-min(off, groups_y - off), off))
    peers_y = {off: (gy + off) % groups_y for off in offsets}

    def for_peers(fn):
        for off_y in offsets:
            for off_x in range(groups_x):
                if off_x or off_y:
                    fn(peers_x[off_x], peers_y[off_y])

    small = (
        pltpu.make_async_copy(old_owner_hbm, old_owner, small_sem.at[0]),
        pltpu.make_async_copy(new_owner_hbm, new_owner, small_sem.at[1]),
        pltpu.make_async_copy(owner_row_hbm, owner_row, small_sem.at[2]),
        pltpu.make_async_copy(count_row, all_counts.at[me], small_sem.at[3]),
    )
    barrier = pltpu.get_barrier_semaphore()
    for off_y in offsets[:-1]:
        pl.semaphore_signal(barrier, inc=1, device_id=(gx, peers_y[off_y]), device_id_type=MESH)
    for off_x in range(1, groups_x):
        pl.semaphore_signal(barrier, inc=1, device_id=(peers_x[off_x], gy), device_id_type=MESH)

    for copy in small:
        copy.start()

    def old_piece(chunk, part):
        state, start, width = pieces[chunk]
        row = pl.multiple_of((part // splits) * SUBLANES, SUBLANES)
        col = pl.multiple_of((part % splits) * span + start, LANES)
        return olds[state].at[:, pl.ds(row, SUBLANES), pl.ds(col, width)]

    def own_rows(chunk):
        return by_rows[chunk].at[pl.ds(gx * held, held)]

    def local_copy(chunk, off):
        target = own_rows(chunk) if off == 0 else ready[chunk].at[off - 1]
        return pltpu.make_async_copy(old_piece(chunk, peers_x[off]), target, local_sem.at[chunk, off])

    def first_copy(chunk, off):
        return pltpu.make_async_remote_copy(
            src_ref=ready[chunk].at[off - 1],
            dst_ref=own_rows(chunk),
            send_sem=send1.at[chunk, off],
            recv_sem=recv1.at[chunk, off],
            device_id=(peers_x[off], gy),
            device_id_type=MESH,
        )

    order = range(chunks)
    for chunk in order:
        for off in [*range(1, groups_x), 0]:
            local_copy(chunk, off).start()

    pl.semaphore_wait(barrier, groups_x + groups_y - 2)
    for off_x in range(1, groups_x):
        pl.semaphore_signal(row_in, inc=1, device_id=(peers_x[off_x], gy), device_id_type=MESH)

    for chunk in order:
        for off in range(1, groups_x):
            local_copy(chunk, off).wait()
            first_copy(chunk, off).start()

    for copy in small:
        copy.wait()

    owners = [new_owner[e] for e in range(experts)]
    places = [old_owner[e] for e in range(experts)]

    def find(slot, carry):
        total = jnp.int32(0)
        for e in range(experts):
            total = total + jnp.where(owners[e] == slot, places[e], 0)
        source[slot] = total
        return carry

    lax.fori_loop(0, experts, find, 0)

    def count_copy(px, py):
        return pltpu.make_async_remote_copy(
            src_ref=count_row,
            dst_ref=all_counts.at[me],
            send_sem=send_c,
            recv_sem=recv_c,
            device_id=(px, py),
            device_id_type=MESH,
        )

    pl.semaphore_wait(row_in, groups_x - 1)
    def landing(chunk):
        state, start, width = pieces[chunk]
        row = pl.multiple_of(gy * rows + (gx // splits) * SUBLANES, SUBLANES)
        col = pl.multiple_of((gx % splits) * span + start, LANES)
        return outs[state].at[0, pl.ds(row, SUBLANES), pl.ds(col, width)]

    def self_copy(chunk):
        return pltpu.make_async_copy(staged[chunk].at[me], landing(chunk), self_sem.at[chunk])

    for chunk in order:
        local_copy(chunk, 0).wait()
        for off in range(1, groups_x):
            first_copy(chunk, off).wait_recv()

        def stage(slot, carry):
            staged[chunk][slot] = by_rows[chunk][source[slot]]
            return carry

        lax.fori_loop(0, experts, stage, 0, unroll=4)

        def send(px, py):
            pltpu.make_async_remote_copy(
                src_ref=staged[chunk].at[px * groups_y + py],
                dst_ref=landing(chunk),
                send_sem=send2.at[chunk],
                recv_sem=recv2.at[chunk],
                device_id=(px, py),
                device_id_type=MESH,
            ).start()

        for_peers(send)
        self_copy(chunk).start()
        if chunk == 0:
            for_peers(lambda px, py: count_copy(px, py).start())

    others = all_counts.at[pl.ds(0, devices - 1)]
    pltpu.make_async_copy(others, others, recv_c).wait()
    totals = jnp.sum(all_counts[...].astype(jnp.float32), axis=0)
    count = jnp.sum(jnp.where(owner_row[...] == me, totals, 0.0), axis=1, keepdims=True)
    count_out[...] = jnp.broadcast_to(count, count_out.shape)

    for chunk in order:
        for off in range(1, groups_x):
            first_copy(chunk, off).wait_send()
    pltpu.make_async_copy(others, others, send_c).wait()
    for chunk in order:
        self_copy(chunk).wait()
        sent = staged[chunk].at[pl.ds(0, devices - 1)]
        pltpu.make_async_copy(sent, sent, send2.at[chunk]).wait()
        pltpu.make_async_copy(sent, sent, recv2.at[chunk]).wait()


def tiled_plan(groups_x, groups_y, shape, experts):
    held, rows, cols = shape
    if rows % SUBLANES or experts != groups_x * groups_y:
        return None
    tiles = rows // SUBLANES
    if groups_x % tiles:
        return None
    span = cols // (groups_x // tiles)
    if span % LANES:
        return None
    half = (span // LANES + 1) // 2 * LANES
    pieces = [(state, 0, half) for state in range(3)]
    if half < span:
        pieces += [(state, half, span - half) for state in range(3)]
    if half > LANES:
        rest = [(state, LANES, half - LANES) for state in range(3)]
        pieces[:3] = [(state, 0, LANES) for state in range(3)] + rest
    return (groups_x, groups_y, experts, held, rows, tiles, span, tuple(pieces))


def kernel_body(dims, old_master, old_first, old_second, new_grad, counts, old_owner, new_owner):
    groups_x, groups_y, experts, held, rows, tiles, span, pieces = dims
    devices = groups_x * groups_y
    chunks = len(pieces)
    tile = (1, rows * groups_y, old_master.shape[2])
    vmem = pl.BlockSpec(memory_space=pltpu.VMEM)
    anywhere = pl.BlockSpec(memory_space=pl.ANY)
    buffers = [pltpu.VMEM((experts, SUBLANES, width), jnp.float32) for _, _, width in pieces] * 2
    buffers += [pltpu.VMEM((groups_x - 1, held, SUBLANES, width), jnp.float32) for _, _, width in pieces]
    row = new_owner.reshape(1, experts)
    operands = (old_owner, new_owner, row, counts.reshape(1, experts), old_master, old_first, old_second)
    kept = [pltpu.with_memory_space_constraint(array, pltpu.HBM) for array in operands]
    master, first, second, count = pl.pallas_call(
        functools.partial(rehome_kernel, dims),
        out_shape=[jax.ShapeDtypeStruct(tile, jnp.float32)] * 3 + [jax.ShapeDtypeStruct((1, LANES), jnp.float32)],
        in_specs=[pl.BlockSpec(memory_space=pltpu.HBM)] * 7,
        out_specs=[anywhere] * 3 + [vmem],
        scratch_shapes=buffers
        + [
            pltpu.SMEM((experts,), jnp.int32),
            pltpu.SMEM((experts,), jnp.int32),
            pltpu.SMEM((experts,), jnp.int32),
            pltpu.VMEM((1, experts), jnp.int32),
            pltpu.VMEM((devices, 1, experts), jnp.int32),
            pltpu.SemaphoreType.DMA((4,)),
            pltpu.SemaphoreType.DMA((chunks, groups_x)),
            pltpu.SemaphoreType.DMA((chunks,)),
            pltpu.SemaphoreType.DMA((chunks, groups_x)),
            pltpu.SemaphoreType.DMA((chunks, groups_x)),
            pltpu.SemaphoreType.DMA((chunks,)),
            pltpu.SemaphoreType.DMA((chunks,)),
            pltpu.SemaphoreType.DMA,
            pltpu.SemaphoreType.DMA,
            pltpu.SemaphoreType.REGULAR,
        ],
        compiler_params=pltpu.CompilerParams(collective_id=0, has_side_effects=True, vmem_limit_bytes=VMEM_GRANT),
    )(*kept)
    return adam_step(master, first, second, new_grad, count[0, 0])


def body(old_master, old_first, old_second, new_grad, counts, old_owner, new_owner):
    dims = tiled_plan(lax.axis_size("gx"), lax.axis_size("gy"), old_master.shape, old_owner.shape[0])
    if dims is None:
        return plain_body(old_master, old_first, old_second, new_grad, counts, old_owner, new_owner)
    return kernel_body(dims, old_master, old_first, old_second, new_grad, counts, old_owner, new_owner)


def solution(mesh):
    placed = (
        P("gx", "gy", None),
        P("gx", "gy", None),
        P("gx", "gy", None),
        P(("gx", "gy"), None, None),
        P(None, ("gx", "gy")),
        P(),
        P(),
    )
    return jax.shard_map(
        body,
        mesh=mesh,
        in_specs=placed,
        out_specs=(P(("gx", "gy"), None, None),) * 3,
        check_vma=False,
    )
```

profile of v0, /device:TPU:0, one launch (start us, length us, event | category | flops | bytes accessed | tf_op | source)
XLA Modules:
  0.0 64.5 jit_solution(4223175562248832508)
XLA Ops:
  0.6 0.0 copy-start
  0.6 62.0 %shard_map.94 = (f32[1,128,1536]{2,1,0:T(8,128)S(1)}, f32[1,128,1536]{2,1,0:T(8,128)S(1)}, f32[1,128,1536]{2,1,0:T(8,128)S(1)}, f32[1,128]{1,0:T(1,128)S(1)}) custom-call(s32[32]{0:T(128)} %old_owner_hbm.1, s32[32]{0:T(128)} %new_owner_hbm.1, s32[1,32]{1,0:T(1,128)} %bitcast.5, s32[1,32]{1,0:T(1,128)} %bitcast.6, f32[8,16,1536]{2,1,0:T(8,128)} %old_m.1, ...), custom_call_target="tpu_custom_call" | custom-call | tf_op jit(solution)/shard_map/pallas_call | solution.py:245
  62.6 0.0 copy-done
  62.7 1.9 %multiply_subtract_fusion = (f32[1,128,1536]{2,1,0:T(8,128)}, f32[1,128,1536]{2,1,0:T(8,128)}, f32[1,128,1536]{2,1,0:T(8,128)}) fusion(f32[1,128,1536]{2,1,0:T(8,128)S(1)} %get-tuple-element.7, f32[]{:T(128)S(1)} %bitcast.4, bf16[1,128,1536]{2,1,0:T(8,128)(2,1)S(1)} %copy-done, f32[1,128,1536]{2,1,0:T(8,128)S(1)} %get-tuple-element.8, ...), kind=kLoop, calls=%fused_computation.2 | loop fusion | flops 3342336 | bytes 5111812 | tf_op jit(solution)/shard_map/sub | solution.py:23
Async XLA Ops:
  0.6 62.0 %copy-start = (bf16[1,128,1536]{2,1,0:T(8,128)(2,1)S(1)}, bf16[1,128,1536]{2,1,0:T(8,128)(2,1)}, u32[]{:S(2)}) copy-start(bf16[1,128,1536]{2,1,0:T(8,128)(2,1)} %param.10) | copy-start | bytes 1179652
where the time goes:
time: 64.7 us; the launch traced here: 64.5 us
  Pallas kernels  62 us (96%)
  other arithmetic  1.86 us (3%)
  between operations  0.66 us (1%)
    pallas_call x1, Pallas kernels, kernel_body(): pl.pallas_call(functools.partial(rehome_kernel, dims), out_shape=[jax.Sha...  62 us
    sub x1, other arithmetic, adam_step(): new_master = master - 0.01 * (step_dir + 0.1 * master)  1.86 us

commit v1 on v0

v1 whole, which is shorter than its diff:
```python
import functools

import jax
import jax.numpy as jnp
from jax import lax
from jax.experimental import pallas as pl
from jax.experimental.pallas import tpu as pltpu
from jax.sharding import PartitionSpec as P

first_correction = 1.0 - 0.9**10
second_correction = 1.0 - 0.999**10
MESH = pl.DeviceIdType.MESH
LANES = 128
VMEM_GRANT = 24 << 20
SUBLANES = 8
PAIR = 2
STATES = 3
ADAM_ROWS = 16
PUBLISHED = 4
HOLD_LOW = 0
HOLD_HIGH = 0
BAND = 2
WIDTHS = (1, 2, 3)


def adam_step(master, first, second, grad, slot_count):
    scaled = grad.astype(jnp.float32) / slot_count
    new_first = 0.9 * first + 0.1 * scaled
    new_second = 0.999 * second + 0.001 * scaled * scaled
    step_dir = new_first / first_correction / (jnp.sqrt(new_second / second_correction) + 1e-08)
    new_master = master - 0.01 * (step_dir + 0.1 * master)
    return (new_master, new_first, new_second)


def adam_scaled(master, first, second, grad, per_token):
    scaled = grad.astype(jnp.float32) * per_token
    new_first = 0.9 * first + 0.1 * scaled
    new_second = 0.999 * second + 0.001 * scaled * scaled
    step_dir = new_first * (1.0 / first_correction) / (jnp.sqrt(new_second * (1.0 / second_correction)) + 1e-08)
    new_master = master - 0.01 * (step_dir + 0.1 * master)
    return (new_master, new_first, new_second)


def reorder(block, groups_x, groups_y):
    total_rows = block.shape[1]
    piece = total_rows // (groups_x * groups_y)
    shaped = block.reshape(1, groups_x, groups_y, piece, block.shape[2])
    return shaped.transpose(0, 2, 1, 3, 4).reshape(1, total_rows, block.shape[2])


def plain_body(old_master, old_first, old_second, new_grad, counts, old_owner, new_owner):
    experts = old_owner.shape[0]
    groups_x = lax.axis_size("gx")
    groups_y = lax.axis_size("gy")
    my_slot = lax.axis_index("gx") * groups_y + lax.axis_index("gy")
    slots = jnp.arange(experts, dtype=jnp.int32)
    onehot = new_owner[:, None] == slots[None, :]
    source = jnp.sum(jnp.where(onehot, old_owner[:, None], 0), axis=0)
    local_counts = counts[:, 0].astype(jnp.float32)
    by_rows = tuple(
        lax.all_to_all(state, "gx", split_axis=1, concat_axis=0, tiled=True)
        for state in (old_master, old_first, old_second)
    )
    permuted = tuple((jnp.take(state, source, axis=0) for state in by_rows))
    landed = lax.all_to_all(permuted, ("gx", "gy"), split_axis=0, concat_axis=1, tiled=True)
    arrived = tuple((reorder(state, groups_x, groups_y) for state in landed))
    totals = lax.psum(local_counts, ("gx", "gy"))
    slot_count = jnp.sum(jnp.where(new_owner == my_slot, totals, jnp.float32(0.0)))
    return adam_step(arrived[0], arrived[1], arrived[2], new_grad, slot_count)


def rehome_kernel(
    plan, old_owner_hbm, new_owner_hbm, owner_row_hbm, count_row, grad_hbm, old_m, old_f, old_s, moved, *scratch
):
    bands = len(plan.widths)
    chunks = bands * STATES
    by_rows = scratch[:chunks]
    staged, ready = scratch[chunks : chunks + bands], scratch[chunks + bands : chunks + 2 * bands]
    (
        source, old_owner, new_owner, owner_row, all_counts, grad,
        small_sem, grad_sem, local_sem, send1, recv1, send2, recv2, send_c, recv_c,
        row_in, up_in, mate_in, far_down, far_up,
    ) = scratch[chunks + 2 * bands :]
    olds = (old_m, old_f, old_s)
    groups_x, groups_y, experts, held, rows = plan.groups_x, plan.groups_y, plan.experts, plan.held, plan.rows
    devices = groups_x * groups_y
    splits = groups_x // plan.tiles
    planes = groups_y // PAIR
    half = planes // 2
    gx = lax.axis_index("gx")
    gy = lax.axis_index("gy")
    me = gx * groups_y + gy
    plane = gy // PAIR
    side = gy % PAIR
    mate = gy + 1 - 2 * side
    upper = plane // half
    has_low = plane > 0
    has_high = plane < planes - 1

    peers_x = [(gx + off) % groups_x for off in range(groups_x)]

    def signal(sem, px, py):
        pl.semaphore_signal(sem, inc=1, device_id=(px, py), device_id_type=MESH)

    barrier = pltpu.get_barrier_semaphore()
    for off in range(1, groups_x):
        signal(barrier, peers_x[off], gy)

    @pl.when(has_high)
    def _():
        signal(barrier, gx, gy + PAIR)
        pl.when(side == 0)(lambda: signal(barrier, gx, mate + PAIR))

    pl.when(side == 0)(lambda: signal(barrier, gx, mate))

    small = (
        pltpu.make_async_copy(old_owner_hbm, old_owner, small_sem),
        pltpu.make_async_copy(new_owner_hbm, new_owner, small_sem),
        pltpu.make_async_copy(owner_row_hbm, owner_row, small_sem),
        pltpu.make_async_copy(count_row, all_counts.at[me], small_sem),
    )
    grad_copy = pltpu.make_async_copy(grad_hbm, grad, grad_sem)

    def landed(ref, sem):
        pltpu.make_async_copy(ref, ref, sem).wait()

    def columns(band, part):
        start = (part % splits) * plan.span + plan.starts[band]
        return pl.ds(pl.multiple_of(start, LANES), plan.widths[band])

    def own_rows(band, state):
        return by_rows[band * STATES + state].at[pl.ds(gx * held, held)]

    def load(band, state, sem):
        for off in [*range(1, groups_x), 0]:
            part = peers_x[off]
            target = own_rows(band, state) if off == 0 else ready[band].at[state, off - 1]
            row = pl.ds(pl.multiple_of((part // splits) * SUBLANES, SUBLANES), SUBLANES)
            pltpu.make_async_copy(olds[state].at[:, row, columns(band, part)], target, sem).start()

    def first_sends(band, state):
        for off in range(1, groups_x):
            pltpu.make_async_remote_copy(
                src_ref=ready[band].at[state, off - 1],
                dst_ref=own_rows(band, state),
                send_sem=send1,
                recv_sem=recv1.at[band * STATES + state],
                device_id=(peers_x[off], gy),
                device_id_type=MESH,
            ).start()

    def loop(start, stop, fn):
        lax.fori_loop(start, stop, lambda k, carry: (fn(k), carry)[1], 0)

    load(0, 0, local_sem.at[0])
    for copy in small:
        copy.start()
    for band in range(bands):
        for state in range(STATES):
            if band or state:
                load(band, state, local_sem.at[1 + band])
    grad_copy.start()

    low = jnp.where(has_low, 1, 0)
    pl.semaphore_wait(barrier, groups_x - 1 + low + side * (1 + low))
    for off in range(1, groups_x):
        signal(row_in, peers_x[off], gy)

    landed(by_rows[0], local_sem.at[0])
    first_sends(0, 0)
    landed(staged[0].at[pl.ds(1, STATES - 1)], local_sem.at[1])
    for state in range(1, STATES):
        first_sends(0, state)
    for band in range(1, bands):
        landed(staged[band], local_sem.at[1 + band])
        for state in range(STATES):
            first_sends(band, state)

    for copy in small:
        copy.wait()
    owners = [new_owner[e] for e in range(experts)]
    places = [old_owner[e] for e in range(experts)]

    def find(slot, carry):
        total = jnp.int32(0)
        for e in range(experts):
            total = total + jnp.where(owners[e] == slot, places[e], 0)
        source[slot] = total
        return carry

    pl.semaphore_wait(row_in, groups_x - 1)
    pl.when(side == 1)(lambda: signal(mate_in, gx, mate))

    lax.fori_loop(0, experts // 2, find, 0)

    pl.when(side == 0)(lambda: pl.semaphore_wait(mate_in, 1))
    pl.when(has_low)(lambda: signal(up_in, gx, gy - PAIR))

    lax.fori_loop(experts // 2, experts, find, 0)

    def meet_upper():
        pl.semaphore_wait(up_in, 1)
        if planes > 2:
            pl.when(has_low)(lambda: signal(far_up.at[0], gx, gy - PAIR))
            pl.when(has_low)(lambda: signal(far_down.at[0], gx, gy + PAIR))

    pl.when(upper == 0)(meet_upper)

    def landing(band, state):
        row = pl.multiple_of(gy * rows + (gx // splits) * SUBLANES, SUBLANES)
        return moved.at[state, pl.ds(row, SUBLANES), columns(band, gx)]

    def send(chunk, px, py):
        band, state = divmod(chunk, STATES)
        pltpu.make_async_remote_copy(
            src_ref=staged[band].at[state, px * groups_y + py],
            dst_ref=landing(band, state),
            send_sem=send2,
            recv_sem=recv2.at[band],
            device_id=(px, py),
            device_id_type=MESH,
        ).start()

    def send_count(px, py):
        pltpu.make_async_remote_copy(
            src_ref=all_counts.at[me],
            dst_ref=all_counts.at[me],
            send_sem=send_c,
            recv_sem=recv_c,
            device_id=(px, py),
            device_id_type=MESH,
        ).start()

    def to_plane(fn, target):
        for pair in range(PAIR):
            py = target * PAIR + (side + pair + 1) % PAIR
            for px in peers_x[1:] + peers_x[:1]:
                fn(px, py)

    def to_own_plane(fn):
        for px in peers_x:
            fn(px, mate)
        for px in peers_x[1:]:
            fn(px, gy)

    def to_distance(fns, far):
        @pl.when(plane >= far)
        def _():
            if far >= 2:
                pl.semaphore_wait(far_down.at[far - 2], 1)
                if far < planes - 1:
                    pl.when(has_high)(lambda: signal(far_down.at[far - 1], gx, gy + PAIR))
            for fn in fns:
                to_plane(fn, plane - far)

        @pl.when(plane < planes - far)
        def _():
            if far >= 2:
                pl.semaphore_wait(far_up.at[far - 2], 1)
                if far < planes - 1:
                    pl.when(has_low)(lambda: signal(far_up.at[far - 1], gx, gy - PAIR))
            for fn in fns:
                to_plane(fn, plane + far)

    def to_known(fn, far):
        for k in range(1, far + 1):
            pl.when(plane >= k)(functools.partial(to_plane, fn, plane - k))
            pl.when(plane < planes - k)(functools.partial(to_plane, fn, plane + k))

    def spread(fn):
        for k in range(half):
            to_plane(fn, upper * k + (1 - upper) * (planes - 1 - k))
        for k in range(1, half):
            to_plane(fn, upper * half + (plane + k) % half)
        to_own_plane(fn)

    def stage(chunk):
        band, state = divmod(chunk, STATES)
        landed(ready[band].at[state], recv1.at[chunk])

        def one(slot, carry):
            staged[band][state, slot] = by_rows[chunk][source[slot]]
            return carry

        lax.fori_loop(0, experts, one, 0, unroll=4)
        landing(band, state)[...] = by_rows[chunk][source[me]]

    early = planes - 1
    for chunk in range(early):
        stage(chunk)
        fn = functools.partial(send, chunk)
        if chunk == 0:
            pl.when(has_low)(lambda: to_plane(fn, plane - 1))
            pl.when(jnp.logical_and(upper == 1, has_high))(meet_upper)
            pl.when(has_high)(lambda: to_plane(fn, plane + 1))
        else:
            to_known(fn, chunk)
            to_distance([functools.partial(send, k) for k in range(chunk + 1)], chunk + 1)
        to_own_plane(fn)

    def step(chunk):
        stage(chunk)
        spread(functools.partial(send, chunk))

    hold = jnp.where(upper == 1, HOLD_LOW, HOLD_HIGH)
    first_plane = (1 - upper) * half

    def eager(chunk):
        stage(chunk)
        fn = functools.partial(send, chunk)
        to_plane(fn, first_plane)
        for k in range(1, half):
            pl.when(chunk < chunks - hold)(functools.partial(to_plane, fn, first_plane + k))
        to_own_plane(fn)
        for k in range(1, half):
            to_plane(fn, upper * half + (plane + k) % half)

    def held_back(chunk):
        for k in range(1, half):
            to_plane(functools.partial(send, chunk), first_plane + k)

    for chunk in range(early, chunks):
        (step if chunk < chunks - max(HOLD_LOW, HOLD_HIGH) else eager)(chunk)
        if chunk == early:
            spread(send_count)
    for chunk in range(chunks - max(HOLD_LOW, HOLD_HIGH), chunks):
        pl.when(chunk >= chunks - hold)(functools.partial(held_back, chunk))

    others = all_counts.at[pl.ds(0, devices - 1)]
    landed(others, recv_c)
    grad_copy.wait()
    totals = jnp.sum(all_counts[...].astype(jnp.float32), axis=0)
    slot_count = jnp.sum(jnp.where(owner_row[...] == me, totals, 0.0), axis=1, keepdims=True)

    per_token = 1.0 / slot_count

    for band, width in enumerate(plan.widths):
        landed(staged[band].at[:, pl.ds(0, devices - 1)], recv2.at[band])

        def adam(step, carry):
            row = pl.ds(pl.multiple_of(step * ADAM_ROWS, ADAM_ROWS), ADAM_ROWS)
            for part in range(splits):
                col = pl.ds(part * plan.span + plan.starts[band], width)
                fresh = adam_scaled(
                    moved[0, row, col], moved[1, row, col], moved[2, row, col], grad[0, row, col], per_token
                )
                for k in range(STATES):
                    moved[k, row, col] = fresh[k]
            return carry

        lax.fori_loop(0, rows * groups_y // ADAM_ROWS, adam, 0, unroll=2)

    landed(others, send_c)
    for band in range(bands):
        landed(ready[band], send1)
        landed(staged[band].at[:, pl.ds(0, devices - 1)], send2)


def publish_kernel(moved, master, first, second, sem):
    rows = master.shape[1] // PUBLISHED
    copies = [
        pltpu.make_async_copy(moved.at[pl.ds(k, 1), pl.ds(part * rows, rows)], out.at[:, pl.ds(part * rows, rows)], sem)
        for k, out in enumerate((master, first, second))
        for part in range(PUBLISHED)
    ]
    for copy in copies:
        copy.start()
    for copy in copies:
        copy.wait()


class Plan:
    def __init__(self, groups_x, groups_y, shape, experts):
        self.groups_x, self.groups_y, self.experts = groups_x, groups_y, experts
        self.held, self.rows, cols = shape
        self.fits = False
        if self.rows % SUBLANES or experts != groups_x * groups_y or groups_y % (2 * PAIR) or groups_y == 2 * PAIR:
            return
        self.tiles = self.rows // SUBLANES
        if groups_x % self.tiles or self.rows * groups_y % ADAM_ROWS:
            return
        self.span = cols // (groups_x // self.tiles)
        if self.span % LANES or cols % (groups_x // self.tiles):
            return
        blocks = self.span // LANES
        widths = [1, *[BAND] * ((blocks - 1) // BAND), (blocks - 1) % BAND]
        widths = WIDTHS if sum(WIDTHS) == blocks else widths
        self.widths = [LANES * width for width in widths if width]
        self.starts = [sum(self.widths[:k]) for k in range(len(self.widths))]
        self.fits = len(self.widths) * STATES > groups_y // PAIR + max(HOLD_LOW, HOLD_HIGH)


def kernel_body(plan, old_master, old_first, old_second, new_grad, counts, old_owner, new_owner):
    experts = plan.experts
    devices = plan.groups_x * plan.groups_y
    bands = len(plan.widths)
    rows, cols = plan.rows * plan.groups_y, old_master.shape[2]
    vmem = pl.BlockSpec(memory_space=pltpu.VMEM)
    hbm = pl.BlockSpec(memory_space=pltpu.HBM)
    far = max(plan.groups_y // PAIR - 2, 1)
    by_rows = [pltpu.VMEM((experts, SUBLANES, width), jnp.float32) for width in plan.widths for _ in range(STATES)]
    staged = [pltpu.VMEM((STATES, experts, SUBLANES, width), jnp.float32) for width in plan.widths]
    ready = [
        pltpu.VMEM((STATES, plan.groups_x - 1, plan.held, SUBLANES, width), jnp.float32) for width in plan.widths
    ]
    row = new_owner.reshape(1, experts)
    operands = (
        old_owner, new_owner, row, counts.reshape(1, experts), new_grad, old_master, old_first, old_second,
    )
    kept = [pltpu.with_memory_space_constraint(array, pltpu.HBM) for array in operands]
    moved = pl.pallas_call(
        functools.partial(rehome_kernel, plan),
        out_shape=jax.ShapeDtypeStruct((STATES, rows, cols), jnp.float32),
        in_specs=[hbm] * 8,
        out_specs=vmem,
        scratch_shapes=by_rows
        + staged
        + ready
        + [
            pltpu.SMEM((experts,), jnp.int32),
            pltpu.SMEM((experts,), jnp.int32),
            pltpu.SMEM((experts,), jnp.int32),
            pltpu.VMEM((1, experts), jnp.int32),
            pltpu.VMEM((devices, 1, experts), jnp.int32),
            pltpu.VMEM((1, rows, cols), new_grad.dtype),
            pltpu.SemaphoreType.DMA,
            pltpu.SemaphoreType.DMA,
            pltpu.SemaphoreType.DMA((bands + 1,)),
            pltpu.SemaphoreType.DMA,
            pltpu.SemaphoreType.DMA((bands * STATES,)),
            pltpu.SemaphoreType.DMA,
            pltpu.SemaphoreType.DMA((bands,)),
            pltpu.SemaphoreType.DMA,
            pltpu.SemaphoreType.DMA,
            pltpu.SemaphoreType.REGULAR,
            pltpu.SemaphoreType.REGULAR,
            pltpu.SemaphoreType.REGULAR,
            pltpu.SemaphoreType.REGULAR((far,)),
            pltpu.SemaphoreType.REGULAR((far,)),
        ],
        compiler_params=pltpu.CompilerParams(collective_id=0, has_side_effects=True, vmem_limit_bytes=VMEM_GRANT),
    )(*kept)
    return pl.pallas_call(
        publish_kernel,
        out_shape=[jax.ShapeDtypeStruct((1, rows, cols), jnp.float32)] * STATES,
        in_specs=[pl.BlockSpec(memory_space=pl.ANY)],
        out_specs=[hbm] * STATES,
        scratch_shapes=[pltpu.SemaphoreType.DMA],
        compiler_params=pltpu.CompilerParams(vmem_limit_bytes=1 << 20),
    )(moved)


def body(old_master, old_first, old_second, new_grad, counts, old_owner, new_owner):
    plan = Plan(lax.axis_size("gx"), lax.axis_size("gy"), old_master.shape, old_owner.shape[0])
    if not plan.fits:
        return plain_body(old_master, old_first, old_second, new_grad, counts, old_owner, new_owner)
    return kernel_body(plan, old_master, old_first, old_second, new_grad, counts, old_owner, new_owner)


def solution(mesh):
    placed = (
        P("gx", "gy", None),
        P("gx", "gy", None),
        P("gx", "gy", None),
        P(("gx", "gy"), None, None),
        P(None, ("gx", "gy")),
        P(),
        P(),
    )
    return jax.shard_map(
        body,
        mesh=mesh,
        in_specs=placed,
        out_specs=(P(("gx", "gy"), None, None),) * 3,
        check_vma=False,
    )
```

time: 64.7 us -> 62.8 us (0.971)
  other arithmetic: 1.86 us -> 0 us
    sub x1 -> x0, other arithmetic: 1.86 us -> none  [adam_step(): new_master = master - 0.01 * (step_dir + 0.1 * master)]
    pallas_call x1 -> x2, Pallas kernels: 62 us -> 62.1 us  [the longest x1 60.7 us: kernel_body(): pl.pallas_call(functools.partial(rehome_kernel, plan), out_shape=jax.Shap...]
where the time goes in v1:
time: 62.8 us; the launch traced here: 62.7 us
  Pallas kernels  62.1 us (99%)
  between operations  0.64 us (1%)
    pallas_call x1, Pallas kernels, kernel_body(): pl.pallas_call(functools.partial(rehome_kernel, plan), out_shape=jax.Shap...  60.7 us
    pallas_call x1, Pallas kernels, kernel_body(): pl.pallas_call(publish_kernel, out_shape=[jax.ShapeDtypeStruct((1, rows,...  1.4 us

profile of v1, /device:TPU:0, one launch (start us, length us, event | category | flops | bytes accessed | tf_op | source)
XLA Modules:
  0.0 62.7 jit_solution(16597330477960337007)
XLA Ops:
  0.6 60.7 %shard_map.94.moved = f32[3,128,1536]{2,1,0:T(8,128)S(1)} custom-call(s32[32]{0:T(128)} %old_owner_hbm.1, s32[32]{0:T(128)} %new_owner_hbm.1, s32[1,32]{1,0:T(1,128)} %bitcast.2, s32[1,32]{1,0:T(1,128)} %bitcast.3, bf16[1,128,1536]{2,1,0:T(8,128)(2,1)} %grad_hbm.1, f32[8,16,1536]{2,1,0:T(8,128)} %old_m.1, f32[8,16,1536]{2,1,0:T(8,128)} %old_f.1, ...), custom_call_target="tpu_custom_call" | custom-call | tf_op jit(solution)/shard_map/pallas_call | solution.py:411
  61.3 1.4 %shard_map.95 = (f32[1,128,1536]{2,1,0:T(8,128)}, f32[1,128,1536]{2,1,0:T(8,128)}, f32[1,128,1536]{2,1,0:T(8,128)}) custom-call(f32[3,128,1536]{2,1,0:T(8,128)S(1)} %shard_map.94.moved), custom_call_target="tpu_custom_call" | custom-call | tf_op jit(solution)/shard_map/pallas_call | solution.py:443

commit v2 on v1

--- a/solution.py
+++ b/solution.py
@@ -15,10 +15,10 @@
 SUBLANES = 8
 PAIR = 2
 STATES = 3
+MASTER, FIRST, SECOND = range(STATES)
+TURNS = (FIRST, SECOND, MASTER)
 ADAM_ROWS = 16
 PUBLISHED = 4
-HOLD_LOW = 0
-HOLD_HIGH = 0
 BAND = 2
 WIDTHS = (1, 2, 3)
 
@@ -32,13 +32,16 @@
     return (new_master, new_first, new_second)
 
 
-def adam_scaled(master, first, second, grad, per_token):
+def adam_direction(first, second, grad, per_token):
     scaled = grad.astype(jnp.float32) * per_token
     new_first = 0.9 * first + 0.1 * scaled
     new_second = 0.999 * second + 0.001 * scaled * scaled
     step_dir = new_first * (1.0 / first_correction) / (jnp.sqrt(new_second * (1.0 / second_correction)) + 1e-08)
-    new_master = master - 0.01 * (step_dir + 0.1 * master)
-    return (new_master, new_first, new_second)
+    return (new_first, new_second, step_dir)
+
+
+def adam_weights(master, step_dir):
+    return master - 0.01 * (step_dir + 0.1 * master)
 
 
 def reorder(block, groups_x, groups_y):
@@ -77,7 +80,7 @@
     by_rows = scratch[:chunks]
     staged, ready = scratch[chunks : chunks + bands], scratch[chunks + bands : chunks + 2 * bands]
     (
-        source, old_owner, new_owner, owner_row, all_counts, grad,
+        source, old_owner, new_owner, owner_row, row_counts, all_counts, grad, steps,
         small_sem, grad_sem, local_sem, send1, recv1, send2, recv2, send_c, recv_c,
         row_in, up_in, mate_in, far_down, far_up,
     ) = scratch[chunks + 2 * bands :]
@@ -117,7 +120,7 @@
         pltpu.make_async_copy(old_owner_hbm, old_owner, small_sem),
         pltpu.make_async_copy(new_owner_hbm, new_owner, small_sem),
         pltpu.make_async_copy(owner_row_hbm, owner_row, small_sem),
-        pltpu.make_async_copy(count_row, all_counts.at[me], small_sem),
+        pltpu.make_async_copy(count_row, row_counts.at[gx], small_sem),
     )
     grad_copy = pltpu.make_async_copy(grad_hbm, grad, grad_sem)
 
@@ -136,7 +139,7 @@
             part = peers_x[off]
             target = own_rows(band, state) if off == 0 else ready[band].at[state, off - 1]
             row = pl.ds(pl.multiple_of((part // splits) * SUBLANES, SUBLANES), SUBLANES)
-            pltpu.make_async_copy(olds[state].at[:, row, columns(band, part)], target, sem).start()
+            pltpu.make_async_copy(olds[TURNS[state]].at[:, row, columns(band, part)], target, sem).start()
 
     def first_sends(band, state):
         for off in range(1, groups_x):
@@ -152,6 +155,16 @@
     def loop(start, stop, fn):
         lax.fori_loop(start, stop, lambda k, carry: (fn(k), carry)[1], 0)
 
+    def count_copy(rows, k, sem, px, py):
+        return pltpu.make_async_remote_copy(
+            src_ref=rows.at[k],
+            dst_ref=rows.at[k],
+            send_sem=send_c.at[sem],
+            recv_sem=recv_c.at[sem],
+            device_id=(px, py),
+            device_id_type=MESH,
+        )
+
     load(0, 0, local_sem.at[0])
     for copy in small:
         copy.start()
@@ -168,6 +181,10 @@
 
     landed(by_rows[0], local_sem.at[0])
     first_sends(0, 0)
+    for copy in small:
+        copy.wait()
+    for off in range(1, groups_x):
+        count_copy(row_counts, gx, 0, peers_x[off], gy).start()
     landed(staged[0].at[pl.ds(1, STATES - 1)], local_sem.at[1])
     for state in range(1, STATES):
         first_sends(0, state)
@@ -176,8 +193,6 @@
         for state in range(STATES):
             first_sends(band, state)
 
-    for copy in small:
-        copy.wait()
     owners = [new_owner[e] for e in range(experts)]
     places = [old_owner[e] for e in range(experts)]
 
@@ -208,7 +223,7 @@
 
     def landing(band, state):
         row = pl.multiple_of(gy * rows + (gx // splits) * SUBLANES, SUBLANES)
-        return moved.at[state, pl.ds(row, SUBLANES), columns(band, gx)]
+        return moved.at[TURNS[state], pl.ds(row, SUBLANES), columns(band, gx)]
 
     def send(chunk, px, py):
         band, state = divmod(chunk, STATES)
@@ -216,20 +231,16 @@
             src_ref=staged[band].at[state, px * groups_y + py],
             dst_ref=landing(band, state),
             send_sem=send2,
-            recv_sem=recv2.at[band],
+            recv_sem=recv2.at[2 * band + state // (STATES - 1)],
             device_id=(px, py),
             device_id_type=MESH,
         ).start()
 
-    def send_count(px, py):
-        pltpu.make_async_remote_copy(
-            src_ref=all_counts.at[me],
-            dst_ref=all_counts.at[me],
-            send_sem=send_c,
-            recv_sem=recv_c,
-            device_id=(px, py),
-            device_id_type=MESH,
-        ).start()
+    def send_counts():
+        landed(row_counts.at[pl.ds(0, groups_x - 1)], recv_c.at[0])
+        all_counts[gy] = jnp.sum(row_counts[...], axis=0)
+        for off in range(1, groups_y):
+            count_copy(all_counts, gy, 1, gx, (gy + off) % groups_y).start()
 
     def to_plane(fn, target):
         for pair in range(PAIR):
@@ -243,29 +254,23 @@
         for px in peers_x[1:]:
             fn(px, gy)
 
-    def to_distance(fns, far):
-        @pl.when(plane >= far)
-        def _():
-            if far >= 2:
-                pl.semaphore_wait(far_down.at[far - 2], 1)
-                if far < planes - 1:
-                    pl.when(has_high)(lambda: signal(far_down.at[far - 1], gx, gy + PAIR))
-            for fn in fns:
-                to_plane(fn, plane - far)
-
-        @pl.when(plane < planes - far)
-        def _():
-            if far >= 2:
-                pl.semaphore_wait(far_up.at[far - 2], 1)
-                if far < planes - 1:
-                    pl.when(has_low)(lambda: signal(far_up.at[far - 1], gx, gy - PAIR))
-            for fn in fns:
-                to_plane(fn, plane + far)
-
-    def to_known(fn, far):
-        for k in range(1, far + 1):
-            pl.when(plane >= k)(functools.partial(to_plane, fn, plane - k))
-            pl.when(plane < planes - k)(functools.partial(to_plane, fn, plane + k))
+    def to_lower(fns, far):
+        pl.semaphore_wait(far_down.at[far - 2], 1)
+        if far < planes - 1:
+            pl.when(has_high)(lambda: signal(far_down.at[far - 1], gx, gy + PAIR))
+        for fn in fns:
+            to_plane(fn, plane - far)
+
+    def reach_down(fn):
+        pl.semaphore_wait(far_down.at[0], 1)
+        to_plane(fn, plane - 2)
+
+    def to_upper(fns, far):
+        pl.semaphore_wait(far_up.at[far - 2], 1)
+        if far < planes - 1:
+            pl.when(has_low)(lambda: signal(far_up.at[far - 1], gx, gy - PAIR))
+        for fn in fns:
+            to_plane(fn, plane + far)
 
     def spread(fn):
         for k in range(half):
@@ -291,66 +296,66 @@
         fn = functools.partial(send, chunk)
         if chunk == 0:
             pl.when(has_low)(lambda: to_plane(fn, plane - 1))
+            pl.when(upper == 1)(functools.partial(reach_down, fn))
             pl.when(jnp.logical_and(upper == 1, has_high))(meet_upper)
+            if planes > 3:
+                pl.when(jnp.logical_and(upper == 1, has_high))(lambda: signal(far_down.at[1], gx, gy + PAIR))
             pl.when(has_high)(lambda: to_plane(fn, plane + 1))
         else:
-            to_known(fn, chunk)
-            to_distance([functools.partial(send, k) for k in range(chunk + 1)], chunk + 1)
+            fns = [functools.partial(send, k) for k in range(chunk + 1)]
+            far = chunk + 1
+            for k in range(1, far):
+                pl.when(plane >= k)(functools.partial(to_plane, fn, plane - k))
+                pl.when(plane < planes - k)(functools.partial(to_plane, fn, plane + k))
+            if far == 2:
+                pl.when(upper == 1)(lambda: to_plane(fn, plane - 2))
+                pl.when(jnp.logical_and(upper == 0, plane >= far))(lambda: to_lower(fns, far))
+            else:
+                pl.when(plane >= far)(lambda: to_lower(fns, far))
+            pl.when(plane < planes - far)(lambda: to_upper(fns, far))
         to_own_plane(fn)
 
     def step(chunk):
         stage(chunk)
         spread(functools.partial(send, chunk))
 
-    hold = jnp.where(upper == 1, HOLD_LOW, HOLD_HIGH)
-    first_plane = (1 - upper) * half
-
-    def eager(chunk):
-        stage(chunk)
-        fn = functools.partial(send, chunk)
-        to_plane(fn, first_plane)
-        for k in range(1, half):
-            pl.when(chunk < chunks - hold)(functools.partial(to_plane, fn, first_plane + k))
-        to_own_plane(fn)
-        for k in range(1, half):
-            to_plane(fn, upper * half + (plane + k) % half)
-
-    def held_back(chunk):
-        for k in range(1, half):
-            to_plane(functools.partial(send, chunk), first_plane + k)
-
     for chunk in range(early, chunks):
-        (step if chunk < chunks - max(HOLD_LOW, HOLD_HIGH) else eager)(chunk)
+        step(chunk)
         if chunk == early:
-            spread(send_count)
-    for chunk in range(chunks - max(HOLD_LOW, HOLD_HIGH), chunks):
-        pl.when(chunk >= chunks - hold)(functools.partial(held_back, chunk))
-
-    others = all_counts.at[pl.ds(0, devices - 1)]
-    landed(others, recv_c)
+            send_counts()
+
+    landed(all_counts.at[pl.ds(0, groups_y - 1)], recv_c.at[1])
     grad_copy.wait()
     totals = jnp.sum(all_counts[...].astype(jnp.float32), axis=0)
     slot_count = jnp.sum(jnp.where(owner_row[...] == me, totals, 0.0), axis=1, keepdims=True)
-
     per_token = 1.0 / slot_count
 
-    for band, width in enumerate(plan.widths):
-        landed(staged[band].at[:, pl.ds(0, devices - 1)], recv2.at[band])
-
-        def adam(step, carry):
+    def tiles(band, fn):
+        def one(step, carry):
             row = pl.ds(pl.multiple_of(step * ADAM_ROWS, ADAM_ROWS), ADAM_ROWS)
             for part in range(splits):
-                col = pl.ds(part * plan.span + plan.starts[band], width)
-                fresh = adam_scaled(
-                    moved[0, row, col], moved[1, row, col], moved[2, row, col], grad[0, row, col], per_token
-                )
-                for k in range(STATES):
-                    moved[k, row, col] = fresh[k]
+                width = plan.widths[band]
+                fn(row, pl.ds(part * plan.span + plan.starts[band], width))
             return carry
 
-        lax.fori_loop(0, rows * groups_y // ADAM_ROWS, adam, 0, unroll=2)
-
-    landed(others, send_c)
+        lax.fori_loop(0, rows * groups_y // ADAM_ROWS, one, 0, unroll=2)
+
+    def moments(row, col):
+        moved[FIRST, row, col], moved[SECOND, row, col], steps[row, col] = adam_direction(
+            moved[FIRST, row, col], moved[SECOND, row, col], grad[0, row, col], per_token
+        )
+
+    def weights(row, col):
+        moved[MASTER, row, col] = adam_weights(moved[MASTER, row, col], steps[row, col])
+
+    for band in range(bands):
+        landed(staged[band].at[pl.ds(0, STATES - 1), pl.ds(0, devices - 1)], recv2.at[2 * band])
+        tiles(band, moments)
+        landed(staged[band].at[0, pl.ds(0, devices - 1)], recv2.at[2 * band + 1])
+        tiles(band, weights)
+
+    landed(row_counts.at[pl.ds(0, groups_x - 1)], send_c.at[0])
+    landed(all_counts.at[pl.ds(0, groups_y - 1)], send_c.at[1])
     for band in range(bands):
         landed(ready[band], send1)
         landed(staged[band].at[:, pl.ds(0, devices - 1)], send2)
@@ -387,7 +392,7 @@
         widths = WIDTHS if sum(WIDTHS) == blocks else widths
         self.widths = [LANES * width for width in widths if width]
         self.starts = [sum(self.widths[:k]) for k in range(len(self.widths))]
-        self.fits = len(self.widths) * STATES > groups_y // PAIR + max(HOLD_LOW, HOLD_HIGH)
+        self.fits = len(self.widths) * STATES > groups_y // PAIR
 
 
 def kernel_body(plan, old_master, old_first, old_second, new_grad, counts, old_owner, new_owner):
@@ -421,17 +426,19 @@
             pltpu.SMEM((experts,), jnp.int32),
             pltpu.SMEM((experts,), jnp.int32),
             pltpu.VMEM((1, experts), jnp.int32),
-            pltpu.VMEM((devices, 1, experts), jnp.int32),
+            pltpu.VMEM((plan.groups_x, 1, experts), jnp.int32),
+            pltpu.VMEM((plan.groups_y, 1, experts), jnp.int32),
             pltpu.VMEM((1, rows, cols), new_grad.dtype),
+            pltpu.VMEM((rows, cols), jnp.float32),
             pltpu.SemaphoreType.DMA,
             pltpu.SemaphoreType.DMA,
             pltpu.SemaphoreType.DMA((bands + 1,)),
             pltpu.SemaphoreType.DMA,
             pltpu.SemaphoreType.DMA((bands * STATES,)),
             pltpu.SemaphoreType.DMA,
-            pltpu.SemaphoreType.DMA((bands,)),
-            pltpu.SemaphoreType.DMA,
-            pltpu.SemaphoreType.DMA,
+            pltpu.SemaphoreType.DMA((2 * bands,)),
+            pltpu.SemaphoreType.DMA((2,)),
+            pltpu.SemaphoreType.DMA((2,)),
             pltpu.SemaphoreType.REGULAR,
             pltpu.SemaphoreType.REGULAR,
             pltpu.SemaphoreType.REGULAR,

time: 62.8 us -> 61.9 us (0.986)
  Pallas kernels: 62.1 us -> 61.1 us
    pallas_call x1, Pallas kernels: 60.7 us -> 59.7 us  [kernel_body(): pl.pallas_call(functools.partial(rehome_kernel, plan), out_shape=jax.Shap...]
where the time goes in v2:
time: 61.9 us; the launch traced here: 61.7 us
  Pallas kernels  61.1 us (99%)
  between operations  0.64 us (1%)
    pallas_call x1, Pallas kernels, kernel_body(): pl.pallas_call(functools.partial(rehome_kernel, plan), out_shape=jax.Shap...  59.7 us
    pallas_call x1, Pallas kernels, kernel_body(): pl.pallas_call(publish_kernel, out_shape=[jax.ShapeDtypeStruct((1, rows,...  1.4 us

profile of v2, /device:TPU:0, one launch (start us, length us, event | category | flops | bytes accessed | tf_op | source)
XLA Modules:
  0.0 61.7 jit_solution(5208427354253433588)
XLA Ops:
  0.6 59.7 %shard_map.94.moved = f32[3,128,1536]{2,1,0:T(8,128)S(1)} custom-call(s32[32]{0:T(128)} %old_owner_hbm.1, s32[32]{0:T(128)} %new_owner_hbm.1, s32[1,32]{1,0:T(1,128)} %bitcast.2, s32[1,32]{1,0:T(1,128)} %bitcast.3, bf16[1,128,1536]{2,1,0:T(8,128)(2,1)} %grad_hbm.1, f32[8,16,1536]{2,1,0:T(8,128)} %old_m.1, f32[8,16,1536]{2,1,0:T(8,128)} %old_f.1, ...), custom_call_target="tpu_custom_call" | custom-call | tf_op jit(solution)/shard_map/pallas_call | solution.py:416
  60.3 1.4 %shard_map.95 = (f32[1,128,1536]{2,1,0:T(8,128)}, f32[1,128,1536]{2,1,0:T(8,128)}, f32[1,128,1536]{2,1,0:T(8,128)}) custom-call(f32[3,128,1536]{2,1,0:T(8,128)S(1)} %shard_map.94.moved), custom_call_target="tpu_custom_call" | custom-call | tf_op jit(solution)/shard_map/pallas_call | solution.py:450

commit v3 on v2

--- a/solution.py
+++ b/solution.py
@@ -1,4 +1,5 @@
 import functools
+from typing import NamedTuple
 
 import jax
 import jax.numpy as jnp
@@ -17,6 +18,8 @@
 STATES = 3
 MASTER, FIRST, SECOND = range(STATES)
 TURNS = (FIRST, SECOND, MASTER)
+FIRST_LOADS = 2
+EARLY_BANDS, LAST_MOMENTS, LAST_WEIGHTS = range(3)
 ADAM_ROWS = 16
 PUBLISHED = 4
 BAND = 2
@@ -75,15 +78,13 @@
 def rehome_kernel(
     plan, old_owner_hbm, new_owner_hbm, owner_row_hbm, count_row, grad_hbm, old_m, old_f, old_s, moved, *scratch
 ):
-    bands = len(plan.widths)
-    chunks = bands * STATES
-    by_rows = scratch[:chunks]
-    staged, ready = scratch[chunks : chunks + bands], scratch[chunks + bands : chunks + 2 * bands]
+    chunks = len(plan.chunks)
+    by_rows, staged, ready = (scratch[k * chunks : (k + 1) * chunks] for k in range(3))
     (
-        source, old_owner, new_owner, owner_row, row_counts, all_counts, grad, steps,
-        small_sem, grad_sem, local_sem, send1, recv1, send2, recv2, send_c, recv_c,
-        row_in, up_in, mate_in, far_down, far_up,
-    ) = scratch[chunks + 2 * bands :]
+        source, old_owner, new_owner, owner_row, row_counts, all_counts, grad, steps, sizes,
+        small_sem, grad_sem, local_sem, sent, recv1, recv2, recv_c,
+        row_in, up_in, mate_in, far_up,
+    ) = scratch[3 * chunks :]
     olds = (old_m, old_f, old_s)
     groups_x, groups_y, experts, held, rows = plan.groups_x, plan.groups_y, plan.experts, plan.held, plan.rows
     devices = groups_x * groups_y
@@ -109,10 +110,12 @@
     for off in range(1, groups_x):
         signal(barrier, peers_x[off], gy)
 
-    @pl.when(has_high)
-    def _():
-        signal(barrier, gx, gy + PAIR)
-        pl.when(side == 0)(lambda: signal(barrier, gx, mate + PAIR))
+    def greet(k):
+        signal(barrier, gx, gy + k * PAIR)
+        pl.when(side == 0)(lambda: signal(barrier, gx, mate + k * PAIR))
+
+    for k in range(1, planes):
+        pl.when(plane + k < planes)(functools.partial(greet, k))
 
     pl.when(side == 0)(lambda: signal(barrier, gx, mate))
 
@@ -127,71 +130,72 @@
     def landed(ref, sem):
         pltpu.make_async_copy(ref, ref, sem).wait()
 
-    def columns(band, part):
-        start = (part % splits) * plan.span + plan.starts[band]
-        return pl.ds(pl.multiple_of(start, LANES), plan.widths[band])
-
-    def own_rows(band, state):
-        return by_rows[band * STATES + state].at[pl.ds(gx * held, held)]
-
-    def load(band, state, sem):
+    def columns(chunk, part):
+        start = (part % splits) * plan.span + plan.chunks[chunk].start
+        return pl.ds(pl.multiple_of(start, LANES), plan.chunks[chunk].width)
+
+    def tile_base(base, part):
+        return pl.multiple_of(base + (part // splits) * SUBLANES, SUBLANES)
+
+    def tile_rows(chunk, base, part):
+        return pl.ds(tile_base(base, part) + plan.chunks[chunk].row, plan.chunks[chunk].rows)
+
+    def own_rows(chunk):
+        return by_rows[chunk].at[pl.ds(gx * held, held)]
+
+    def load(chunk):
+        state = plan.chunks[chunk].state
         for off in [*range(1, groups_x), 0]:
             part = peers_x[off]
-            target = own_rows(band, state) if off == 0 else ready[band].at[state, off - 1]
-            row = pl.ds(pl.multiple_of((part // splits) * SUBLANES, SUBLANES), SUBLANES)
-            pltpu.make_async_copy(olds[TURNS[state]].at[:, row, columns(band, part)], target, sem).start()
-
-    def first_sends(band, state):
+            target = own_rows(chunk) if off == 0 else ready[chunk].at[off - 1]
+            piece = olds[state].at[:, tile_rows(chunk, 0, part), columns(chunk, part)]
+            pltpu.make_async_copy(piece, target, local_sem.at[0 if chunk < FIRST_LOADS else 1]).start()
+
+    def first_sends(chunk):
         for off in range(1, groups_x):
             pltpu.make_async_remote_copy(
-                src_ref=ready[band].at[state, off - 1],
-                dst_ref=own_rows(band, state),
-                send_sem=send1,
-                recv_sem=recv1.at[band * STATES + state],
+                src_ref=ready[chunk].at[off - 1],
+                dst_ref=own_rows(chunk),
+                send_sem=sent,
+                recv_sem=recv1.at[chunk],
                 device_id=(peers_x[off], gy),
                 device_id_type=MESH,
             ).start()
-
-    def loop(start, stop, fn):
-        lax.fori_loop(start, stop, lambda k, carry: (fn(k), carry)[1], 0)
 
     def count_copy(rows, k, sem, px, py):
         return pltpu.make_async_remote_copy(
             src_ref=rows.at[k],
             dst_ref=rows.at[k],
-            send_sem=send_c.at[sem],
+            send_sem=sent,
             recv_sem=recv_c.at[sem],
             device_id=(px, py),
             device_id_type=MESH,
         )
 
-    load(0, 0, local_sem.at[0])
+    for chunk in range(FIRST_LOADS):
+        load(chunk)
     for copy in small:
         copy.start()
-    for band in range(bands):
-        for state in range(STATES):
-            if band or state:
-                load(band, state, local_sem.at[1 + band])
+    for chunk in range(FIRST_LOADS, chunks):
+        load(chunk)
     grad_copy.start()
 
-    low = jnp.where(has_low, 1, 0)
-    pl.semaphore_wait(barrier, groups_x - 1 + low + side * (1 + low))
+    pl.semaphore_wait(barrier, groups_x - 1 + plane * (1 + side) + side)
     for off in range(1, groups_x):
         signal(row_in, peers_x[off], gy)
 
-    landed(by_rows[0], local_sem.at[0])
-    first_sends(0, 0)
+    for chunk in range(FIRST_LOADS):
+        landed(by_rows[chunk], local_sem.at[0])
+    for chunk in range(FIRST_LOADS):
+        first_sends(chunk)
     for copy in small:
         copy.wait()
     for off in range(1, groups_x):
         count_copy(row_counts, gx, 0, peers_x[off], gy).start()
-    landed(staged[0].at[pl.ds(1, STATES - 1)], local_sem.at[1])
-    for state in range(1, STATES):
-        first_sends(0, state)
-    for band in range(1, bands):
-        landed(staged[band], local_sem.at[1 + band])
-        for state in range(STATES):
-            first_sends(band, state)
+    for chunk in range(FIRST_LOADS, chunks):
+        landed(by_rows[chunk], local_sem.at[1])
+    for chunk in range(FIRST_LOADS, chunks):
+        first_sends(chunk)
 
     owners = [new_owner[e] for e in range(experts)]
     places = [old_owner[e] for e in range(experts)]
@@ -204,34 +208,36 @@
         return carry
 
     pl.semaphore_wait(row_in, groups_x - 1)
-    pl.when(side == 1)(lambda: signal(mate_in, gx, mate))
-
-    lax.fori_loop(0, experts // 2, find, 0)
+
+    @pl.when(side == 1)
+    def _():
+        signal(mate_in, gx, mate)
+
+        @pl.when(has_low)
+        def _():
+            signal(up_in, gx, gy - PAIR)
+            signal(up_in, gx, mate - PAIR)
+
+    lax.fori_loop(0, experts, find, 0)
 
     pl.when(side == 0)(lambda: pl.semaphore_wait(mate_in, 1))
-    pl.when(has_low)(lambda: signal(up_in, gx, gy - PAIR))
-
-    lax.fori_loop(experts // 2, experts, find, 0)
 
     def meet_upper():
         pl.semaphore_wait(up_in, 1)
         if planes > 2:
             pl.when(has_low)(lambda: signal(far_up.at[0], gx, gy - PAIR))
-            pl.when(has_low)(lambda: signal(far_down.at[0], gx, gy + PAIR))
 
     pl.when(upper == 0)(meet_upper)
 
-    def landing(band, state):
-        row = pl.multiple_of(gy * rows + (gx // splits) * SUBLANES, SUBLANES)
-        return moved.at[TURNS[state], pl.ds(row, SUBLANES), columns(band, gx)]
+    def landing(chunk):
+        return moved.at[plan.chunks[chunk].state, tile_rows(chunk, gy * rows, gx), columns(chunk, gx)]
 
     def send(chunk, px, py):
-        band, state = divmod(chunk, STATES)
         pltpu.make_async_remote_copy(
-            src_ref=staged[band].at[state, px * groups_y + py],
-            dst_ref=landing(band, state),
-            send_sem=send2,
-            recv_sem=recv2.at[2 * band + state // (STATES - 1)],
+            src_ref=staged[chunk].at[px * groups_y + py],
+            dst_ref=landing(chunk),
+            send_sem=sent,
+            recv_sem=recv2.at[plan.chunks[chunk].lands],
             device_id=(px, py),
             device_id_type=MESH,
         ).start()
@@ -253,17 +259,6 @@
             fn(px, mate)
         for px in peers_x[1:]:
             fn(px, gy)
-
-    def to_lower(fns, far):
-        pl.semaphore_wait(far_down.at[far - 2], 1)
-        if far < planes - 1:
-            pl.when(has_high)(lambda: signal(far_down.at[far - 1], gx, gy + PAIR))
-        for fn in fns:
-            to_plane(fn, plane - far)
-
-    def reach_down(fn):
-        pl.semaphore_wait(far_down.at[0], 1)
-        to_plane(fn, plane - 2)
 
     def to_upper(fns, far):
         pl.semaphore_wait(far_up.at[far - 2], 1)
@@ -280,39 +275,37 @@
         to_own_plane(fn)
 
     def stage(chunk):
-        band, state = divmod(chunk, STATES)
-        landed(ready[band].at[state], recv1.at[chunk])
+        landed(ready[chunk], recv1.at[chunk])
 
         def one(slot, carry):
-            staged[band][state, slot] = by_rows[chunk][source[slot]]
+            staged[chunk][slot] = by_rows[chunk][source[slot]]
             return carry
 
         lax.fori_loop(0, experts, one, 0, unroll=4)
-        landing(band, state)[...] = by_rows[chunk][source[me]]
-
-    early = planes - 1
+        if chunk >= FIRST_LOADS:
+            landing(chunk)[...] = by_rows[chunk][source[me]]
+        elif chunk == FIRST_LOADS - 1:
+            own = [by_rows[k][source[me]] for k in range(FIRST_LOADS)]
+            moved[TURNS[0], pl.ds(tile_base(gy * rows, gx), SUBLANES), columns(0, gx)] = jnp.concatenate(own)
+
+    opening = {far: FIRST_LOADS + far - 2 for far in range(2, planes)}
+    early = opening[planes - 1] + 1
     for chunk in range(early):
         stage(chunk)
         fn = functools.partial(send, chunk)
+        pl.when(upper == 0)(functools.partial(to_plane, fn, plane + 1))
+        for k in range(1, planes):
+            pl.when(plane >= k)(functools.partial(to_plane, fn, plane - k))
+        above = jnp.logical_and(upper == 1, has_high)
         if chunk == 0:
-            pl.when(has_low)(lambda: to_plane(fn, plane - 1))
-            pl.when(upper == 1)(functools.partial(reach_down, fn))
-            pl.when(jnp.logical_and(upper == 1, has_high))(meet_upper)
-            if planes > 3:
-                pl.when(jnp.logical_and(upper == 1, has_high))(lambda: signal(far_down.at[1], gx, gy + PAIR))
-            pl.when(has_high)(lambda: to_plane(fn, plane + 1))
-        else:
-            fns = [functools.partial(send, k) for k in range(chunk + 1)]
-            far = chunk + 1
-            for k in range(1, far):
-                pl.when(plane >= k)(functools.partial(to_plane, fn, plane - k))
-                pl.when(plane < planes - k)(functools.partial(to_plane, fn, plane + k))
-            if far == 2:
-                pl.when(upper == 1)(lambda: to_plane(fn, plane - 2))
-                pl.when(jnp.logical_and(upper == 0, plane >= far))(lambda: to_lower(fns, far))
-            else:
-                pl.when(plane >= far)(lambda: to_lower(fns, far))
-            pl.when(plane < planes - far)(lambda: to_upper(fns, far))
+            pl.when(above)(meet_upper)
+        pl.when(above)(functools.partial(to_plane, fn, plane + 1))
+        for far, opens in opening.items():
+            if chunk > opens:
+                pl.when(plane < planes - far)(functools.partial(to_plane, fn, plane + far))
+            if chunk == opens:
+                fns = [functools.partial(send, k) for k in range(chunk + 1)]
+                pl.when(plane < planes - far)(functools.partial(to_upper, fns, far))
         to_own_plane(fn)
 
     def step(chunk):
@@ -330,12 +323,11 @@
     slot_count = jnp.sum(jnp.where(owner_row[...] == me, totals, 0.0), axis=1, keepdims=True)
     per_token = 1.0 / slot_count
 
-    def tiles(band, fn):
+    def tiles(start, width, fn):
         def one(step, carry):
             row = pl.ds(pl.multiple_of(step * ADAM_ROWS, ADAM_ROWS), ADAM_ROWS)
             for part in range(splits):
-                width = plan.widths[band]
-                fn(row, pl.ds(part * plan.span + plan.starts[band], width))
+                fn(row, pl.ds(part * plan.span + start, width))
             return carry
 
         lax.fori_loop(0, rows * groups_y // ADAM_ROWS, one, 0, unroll=2)
@@ -348,17 +340,24 @@
     def weights(row, col):
         moved[MASTER, row, col] = adam_weights(moved[MASTER, row, col], steps[row, col])
 
-    for band in range(bands):
-        landed(staged[band].at[pl.ds(0, STATES - 1), pl.ds(0, devices - 1)], recv2.at[2 * band])
-        tiles(band, moments)
-        landed(staged[band].at[0, pl.ds(0, devices - 1)], recv2.at[2 * band + 1])
-        tiles(band, weights)
-
-    landed(row_counts.at[pl.ds(0, groups_x - 1)], send_c.at[0])
-    landed(all_counts.at[pl.ds(0, groups_y - 1)], send_c.at[1])
-    for band in range(bands):
-        landed(ready[band], send1)
-        landed(staged[band].at[:, pl.ds(0, devices - 1)], send2)
+    def all_landed(group, states, width):
+        landed(sizes.at[:, :, pl.ds(0, states * width)], recv2.at[group])
+
+    last_start, last_width = plan.bands[-1]
+    all_landed(EARLY_BANDS, STATES, last_start)
+    for start, width in plan.bands[:-1]:
+        tiles(start, width, moments)
+        tiles(start, width, weights)
+    all_landed(LAST_MOMENTS, STATES - 1, last_width)
+    tiles(last_start, last_width, moments)
+    all_landed(LAST_WEIGHTS, 1, last_width)
+    tiles(last_start, last_width, weights)
+
+    landed(row_counts.at[pl.ds(0, groups_x - 1)], sent)
+    landed(all_counts.at[pl.ds(0, groups_y - 1)], sent)
+    for chunk in range(chunks):
+        landed(ready[chunk], sent)
+        landed(staged[chunk].at[pl.ds(0, devices - 1)], sent)
 
 
 def publish_kernel(moved, master, first, second, sem):
@@ -372,6 +371,15 @@
         copy.start()
     for copy in copies:
         copy.wait()
+
+
+class Chunk(NamedTuple):
+    state: int
+    start: int
+    width: int
+    row: int
+    rows: int
+    lands: int
 
 
 class Plan:
@@ -389,24 +397,32 @@
             return
         blocks = self.span // LANES
         widths = [1, *[BAND] * ((blocks - 1) // BAND), (blocks - 1) % BAND]
-        widths = WIDTHS if sum(WIDTHS) == blocks else widths
-        self.widths = [LANES * width for width in widths if width]
-        self.starts = [sum(self.widths[:k]) for k in range(len(self.widths))]
-        self.fits = len(self.widths) * STATES > groups_y // PAIR
+        widths = WIDTHS if sum(WIDTHS) == blocks else [width for width in widths if width]
+        self.bands = [(LANES * sum(widths[:k]), LANES * width) for k, width in enumerate(widths)]
+        self.chunks = []
+        for start, width in self.bands:
+            for state in TURNS:
+                lands = EARLY_BANDS
+                if (start, width) == self.bands[-1]:
+                    lands = LAST_WEIGHTS if state == MASTER else LAST_MOMENTS
+                pieces = FIRST_LOADS if not self.chunks else 1
+                for k in range(pieces):
+                    size = SUBLANES // pieces
+                    self.chunks.append(Chunk(state, start, width, k * size, size, lands))
+        self.fits = len(widths) > 1 and len(self.chunks) > FIRST_LOADS + groups_y // PAIR
 
 
 def kernel_body(plan, old_master, old_first, old_second, new_grad, counts, old_owner, new_owner):
     experts = plan.experts
     devices = plan.groups_x * plan.groups_y
-    bands = len(plan.widths)
+    chunks = len(plan.chunks)
     rows, cols = plan.rows * plan.groups_y, old_master.shape[2]
     vmem = pl.BlockSpec(memory_space=pltpu.VMEM)
     hbm = pl.BlockSpec(memory_space=pltpu.HBM)
     far = max(plan.groups_y // PAIR - 2, 1)
-    by_rows = [pltpu.VMEM((experts, SUBLANES, width), jnp.float32) for width in plan.widths for _ in range(STATES)]
-    staged = [pltpu.VMEM((STATES, experts, SUBLANES, width), jnp.float32) for width in plan.widths]
+    by_rows = [pltpu.VMEM((experts, chunk.rows, chunk.width), jnp.float32) for chunk in plan.chunks]
     ready = [
-        pltpu.VMEM((STATES, plan.groups_x - 1, plan.held, SUBLANES, width), jnp.float32) for width in plan.widths
+        pltpu.VMEM((plan.groups_x - 1, plan.held, chunk.rows, chunk.width), jnp.float32) for chunk in plan.chunks
     ]
     row = new_owner.reshape(1, experts)
     operands = (
@@ -418,8 +434,7 @@
         out_shape=jax.ShapeDtypeStruct((STATES, rows, cols), jnp.float32),
         in_specs=[hbm] * 8,
         out_specs=vmem,
-        scratch_shapes=by_rows
-        + staged
+        scratch_shapes=by_rows * 2
         + ready
         + [
             pltpu.SMEM((experts,), jnp.int32),
@@ -430,19 +445,17 @@
             pltpu.VMEM((plan.groups_y, 1, experts), jnp.int32),
             pltpu.VMEM((1, rows, cols), new_grad.dtype),
             pltpu.VMEM((rows, cols), jnp.float32),
+            pltpu.VMEM((devices - 1, SUBLANES, STATES * plan.span), jnp.float32),
             pltpu.SemaphoreType.DMA,
             pltpu.SemaphoreType.DMA,
-            pltpu.SemaphoreType.DMA((bands + 1,)),
+            pltpu.SemaphoreType.DMA((2,)),
             pltpu.SemaphoreType.DMA,
-            pltpu.SemaphoreType.DMA((bands * STATES,)),
-            pltpu.SemaphoreType.DMA,
-            pltpu.SemaphoreType.DMA((2 * bands,)),
-            pltpu.SemaphoreType.DMA((2,)),
+            pltpu.SemaphoreType.DMA((chunks,)),
+            pltpu.SemaphoreType.DMA((3,)),
             pltpu.SemaphoreType.DMA((2,)),
             pltpu.SemaphoreType.REGULAR,
             pltpu.SemaphoreType.REGULAR,
             pltpu.SemaphoreType.REGULAR,
-            pltpu.SemaphoreType.REGULAR((far,)),
             pltpu.SemaphoreType.REGULAR((far,)),
         ],
         compiler_params=pltpu.CompilerParams(collective_id=0, has_side_effects=True, vmem_limit_bytes=VMEM_GRANT),

time: 61.9 us -> 61.4 us (level)
  no operation moved by 1% of the time
where the time goes in v3:
time: 61.4 us; the launch traced here: 61.3 us
  Pallas kernels  60.6 us (99%)
  between operations  0.64 us (1%)
    pallas_call x1, Pallas kernels, kernel_body(): pl.pallas_call(functools.partial(rehome_kernel, plan), out_shape=jax.Shap...  59.2 us
    pallas_call x1, Pallas kernels, kernel_body(): pl.pallas_call(publish_kernel, out_shape=[jax.ShapeDtypeStruct((1, rows,...  1.4 us

profile of v3, /device:TPU:0, one launch (start us, length us, event | category | flops | bytes accessed | tf_op | source)
XLA Modules:
  0.0 61.3 jit_solution(15703603399512534466)
XLA Ops:
  0.6 59.2 %shard_map.94.moved = f32[3,128,1536]{2,1,0:T(8,128)S(1)} custom-call(s32[32]{0:T(128)} %old_owner_hbm.1, s32[32]{0:T(128)} %new_owner_hbm.1, s32[1,32]{1,0:T(1,128)} %bitcast.2, s32[1,32]{1,0:T(1,128)} %bitcast.3, bf16[1,128,1536]{2,1,0:T(8,128)(2,1)} %grad_hbm.1, f32[8,16,1536]{2,1,0:T(8,128)} %old_m.1, f32[8,16,1536]{2,1,0:T(8,128)} %old_f.1, ...), custom_call_target="tpu_custom_call" | custom-call | tf_op jit(solution)/shard_map/pallas_call | solution.py:432
  59.9 1.4 %shard_map.95 = (f32[1,128,1536]{2,1,0:T(8,128)}, f32[1,128,1536]{2,1,0:T(8,128)}, f32[1,128,1536]{2,1,0:T(8,128)}) custom-call(f32[3,128,1536]{2,1,0:T(8,128)S(1)} %shard_map.94.moved), custom_call_target="tpu_custom_call" | custom-call | tf_op jit(solution)/shard_map/pallas_call | solution.py:463

commit v4 on v3

--- a/solution.py
+++ b/solution.py
@@ -15,6 +15,7 @@
 VMEM_GRANT = 24 << 20
 SUBLANES = 8
 PAIR = 2
+CORES = 2
 STATES = 3
 MASTER, FIRST, SECOND = range(STATES)
 TURNS = (FIRST, SECOND, MASTER)
@@ -101,7 +102,11 @@
     has_low = plane > 0
     has_high = plane < planes - 1
 
-    peers_x = [(gx + off) % groups_x for off in range(groups_x)]
+    core = gx % CORES
+    peers_x = [gx]
+    for k in range(1, groups_x // CORES):
+        peers_x += [(gx - core + CORES * k) % groups_x + CORES - 1 - c for c in range(CORES)]
+    peers_x += [gx - core + (core + k) % CORES for k in range(1, CORES)]
 
     def signal(sem, px, py):
         pl.semaphore_signal(sem, inc=1, device_id=(px, py), device_id_type=MESH)
@@ -266,6 +271,31 @@
             pl.when(has_low)(lambda: signal(far_up.at[far - 1], gx, gy - PAIR))
         for fn in fns:
             to_plane(fn, plane + far)
+
+    def spread_last(fn):
+        row = CORES
+        corner = [(0, px) for px in reversed(range(row))]
+        rest = [(pair, px) for px in range(groups_x) for pair in range(PAIR) if (pair, px) not in corner]
+
+        def to_part(target, part):
+            for pair, px in part:
+                fn(px, target * PAIR + pair)
+
+        def downward():
+            for part in (corner, rest):
+                for target in range(half):
+                    to_part(target, part)
+
+        def upward():
+            for part in (corner, rest):
+                for target in range(half, planes):
+                    to_part(target, part)
+
+        pl.when(upper == 1)(downward)
+        pl.when(upper == 0)(upward)
+        for k in range(1, half):
+            to_plane(fn, upper * half + (plane + k) % half)
+        to_own_plane(fn)
 
     def spread(fn):
         for k in range(half):
@@ -310,7 +340,7 @@
 
     def step(chunk):
         stage(chunk)
-        spread(functools.partial(send, chunk))
+        (spread_last if chunk == chunks - 1 else spread)(functools.partial(send, chunk))
 
     for chunk in range(early, chunks):
         step(chunk)
@@ -387,7 +417,7 @@
         self.groups_x, self.groups_y, self.experts = groups_x, groups_y, experts
         self.held, self.rows, cols = shape
         self.fits = False
-        if self.rows % SUBLANES or experts != groups_x * groups_y or groups_y % (2 * PAIR) or groups_y == 2 * PAIR:
+        if self.rows % SUBLANES or experts != groups_x * groups_y or groups_x % CORES or groups_y % (2 * PAIR) or groups_y == 2 * PAIR:
             return
         self.tiles = self.rows // SUBLANES
         if groups_x % self.tiles or self.rows * groups_y % ADAM_ROWS:

time: 61.4 us -> 61.2 us (level); the launches traced: 61.3 us -> 60.1 us
  Pallas kernels: 60.6 us -> 59.5 us
    pallas_call x1, Pallas kernels: 59.2 us -> 58.1 us  [kernel_body(): pl.pallas_call(functools.partial(rehome_kernel, plan), out_shape=jax.Shap...]
where the time goes in v4:
time: 61.2 us; the launch traced here: 60.1 us
  Pallas kernels  59.5 us (97%)
  between operations  0.64 us (1%)
    pallas_call x1, Pallas kernels, kernel_body(): pl.pallas_call(functools.partial(rehome_kernel, plan), out_shape=jax.Shap...  58.1 us
    pallas_call x1, Pallas kernels, kernel_body(): pl.pallas_call(publish_kernel, out_shape=[jax.ShapeDtypeStruct((1, rows,...  1.4 us

profile of v4, /device:TPU:0, one launch (start us, length us, event | category | flops | bytes accessed | tf_op | source)
XLA Modules:
  0.0 60.1 jit_solution(1428753183185662801)
XLA Ops:
  0.6 58.1 %shard_map.94.moved = f32[3,128,1536]{2,1,0:T(8,128)S(1)} custom-call(s32[32]{0:T(128)} %old_owner_hbm.1, s32[32]{0:T(128)} %new_owner_hbm.1, s32[1,32]{1,0:T(1,128)} %bitcast.2, s32[1,32]{1,0:T(1,128)} %bitcast.3, bf16[1,128,1536]{2,1,0:T(8,128)(2,1)} %grad_hbm.1, f32[8,16,1536]{2,1,0:T(8,128)} %old_m.1, f32[8,16,1536]{2,1,0:T(8,128)} %old_f.1, ...), custom_call_target="tpu_custom_call" | custom-call | tf_op jit(solution)/shard_map/pallas_call | solution.py:462
  58.7 1.4 %shard_map.95 = (f32[1,128,1536]{2,1,0:T(8,128)}, f32[1,128,1536]{2,1,0:T(8,128)}, f32[1,128,1536]{2,1,0:T(8,128)}) custom-call(f32[3,128,1536]{2,1,0:T(8,128)S(1)} %shard_map.94.moved), custom_call_target="tpu_custom_call" | custom-call | tf_op jit(solution)/shard_map/pallas_call | solution.py:493

commit v5 on v4

--- a/solution.py
+++ b/solution.py
@@ -19,7 +19,7 @@
 STATES = 3
 MASTER, FIRST, SECOND = range(STATES)
 TURNS = (FIRST, SECOND, MASTER)
-FIRST_LOADS = 2
+FIRST_LOADS = 4
 EARLY_BANDS, LAST_MOMENTS, LAST_WEIGHTS = range(3)
 ADAM_ROWS = 16
 PUBLISHED = 4
@@ -275,7 +275,7 @@
     def spread_last(fn):
         row = CORES
         corner = [(0, px) for px in reversed(range(row))]
-        rest = [(pair, px) for px in range(groups_x) for pair in range(PAIR) if (pair, px) not in corner]
+        rest = [(pair, px) for pair in range(PAIR) for px in range(groups_x) if (pair, px) not in corner]
 
         def to_part(target, part):
             for pair, px in part:

time: 61.2 us -> 60.9 us (level)
  no operation moved by 1% of the time
where the time goes in v5:
time: 60.9 us; the launch traced here: 60.2 us
  Pallas kernels  59.5 us (98%)
  between operations  0.64 us (1%)
    pallas_call x1, Pallas kernels, kernel_body(): pl.pallas_call(functools.partial(rehome_kernel, plan), out_shape=jax.Shap...  58.1 us
    pallas_call x1, Pallas kernels, kernel_body(): pl.pallas_call(publish_kernel, out_shape=[jax.ShapeDtypeStruct((1, rows,...  1.4 us

profile of v5, /device:TPU:0, one launch (start us, length us, event | category | flops | bytes accessed | tf_op | source)
XLA Modules:
  0.0 60.2 jit_solution(16220230913196022922)
XLA Ops:
  0.6 58.1 %shard_map.94.moved = f32[3,128,1536]{2,1,0:T(8,128)S(1)} custom-call(s32[32]{0:T(128)} %old_owner_hbm.1, s32[32]{0:T(128)} %new_owner_hbm.1, s32[1,32]{1,0:T(1,128)} %bitcast.2, s32[1,32]{1,0:T(1,128)} %bitcast.3, bf16[1,128,1536]{2,1,0:T(8,128)(2,1)} %grad_hbm.1, f32[8,16,1536]{2,1,0:T(8,128)} %old_m.1, f32[8,16,1536]{2,1,0:T(8,128)} %old_f.1, ...), custom_call_target="tpu_custom_call" | custom-call | tf_op jit(solution)/shard_map/pallas_call | solution.py:462
  58.8 1.4 %shard_map.95 = (f32[1,128,1536]{2,1,0:T(8,128)}, f32[1,128,1536]{2,1,0:T(8,128)}, f32[1,128,1536]{2,1,0:T(8,128)}) custom-call(f32[3,128,1536]{2,1,0:T(8,128)S(1)} %shard_map.94.moved), custom_call_target="tpu_custom_call" | custom-call | tf_op jit(solution)/shard_map/pallas_call | solution.py:493

commit v6 on v5

--- a/solution.py
+++ b/solution.py
@@ -318,7 +318,7 @@
             own = [by_rows[k][source[me]] for k in range(FIRST_LOADS)]
             moved[TURNS[0], pl.ds(tile_base(gy * rows, gx), SUBLANES), columns(0, gx)] = jnp.concatenate(own)
 
-    opening = {far: FIRST_LOADS + far - 2 for far in range(2, planes)}
+    opening = {far: FIRST_LOADS + far - 3 for far in range(2, planes)}
     early = opening[planes - 1] + 1
     for chunk in range(early):
         stage(chunk)

time: 60.9 us -> 61 us (level)
  no operation moved by 1% of the time
where the time goes in v6:
time: 61 us; the launch traced here: 60.2 us
  Pallas kernels  59.6 us (98%)
  between operations  0.64 us (1%)
    pallas_call x1, Pallas kernels, kernel_body(): pl.pallas_call(functools.partial(rehome_kernel, plan), out_shape=jax.Shap...  58.2 us
    pallas_call x1, Pallas kernels, kernel_body(): pl.pallas_call(publish_kernel, out_shape=[jax.ShapeDtypeStruct((1, rows,...  1.4 us

profile of v6, /device:TPU:0, one launch (start us, length us, event | category | flops | bytes accessed | tf_op | source)
XLA Modules:
  0.0 60.2 jit_solution(7208753146256928343)
XLA Ops:
  0.6 58.2 %shard_map.94.moved = f32[3,128,1536]{2,1,0:T(8,128)S(1)} custom-call(s32[32]{0:T(128)} %old_owner_hbm.1, s32[32]{0:T(128)} %new_owner_hbm.1, s32[1,32]{1,0:T(1,128)} %bitcast.2, s32[1,32]{1,0:T(1,128)} %bitcast.3, bf16[1,128,1536]{2,1,0:T(8,128)(2,1)} %grad_hbm.1, f32[8,16,1536]{2,1,0:T(8,128)} %old_m.1, f32[8,16,1536]{2,1,0:T(8,128)} %old_f.1, ...), custom_call_target="tpu_custom_call" | custom-call | tf_op jit(solution)/shard_map/pallas_call | solution.py:462
  58.8 1.4 %shard_map.95 = (f32[1,128,1536]{2,1,0:T(8,128)}, f32[1,128,1536]{2,1,0:T(8,128)}, f32[1,128,1536]{2,1,0:T(8,128)}) custom-call(f32[3,128,1536]{2,1,0:T(8,128)S(1)} %shard_map.94.moved), custom_call_target="tpu_custom_call" | custom-call | tf_op jit(solution)/shard_map/pallas_call | solution.py:493
